TPU v7x, 256 devices: a whole 4x4x8 slice. The times are simulated.
256 devices in a mesh: dp: 16 (over y, x_hi, core), tensor: 16 (over x_lo, z).
Axes of the slice: x: 4 (x_hi: 2, x_lo: 2; x = x_hi * 2 + x_lo), y: 4, z: 8, core: 2. Of those that a mesh axis runs over, the one named last changes fastest.
Arguments:
- tokens: bfloat16 [32768, 2304], P(('dp', 'tensor')), may hold values from -6 to 6
- cotangent: bfloat16 [32768, 4096], P('dp', 'tensor'), may hold values from -6 to 6
- pre_gain: float32 [2304], replicated, may hold values from 0.25 to 1.75
- w_query: bfloat16 [2304, 4096], P('dp', 'tensor'), may hold values from -0.375 to 0.375
- key_weight: bfloat16 [2304, 2048], P('dp', 'tensor'), may hold values from -0.375 to 0.375
- value_weight: bfloat16 [2304, 2048], P('dp', 'tensor'), may hold values from -0.125 to 0.125
Outputs:
- attended: bfloat16 [32768, 4096], P('dp', 'tensor')
- grad_tokens: bfloat16 [32768, 2304], P(('dp', 'tensor'))
- grad_query: float32 [2304, 4096], P('dp', 'tensor')
- grad_key: float32 [2304, 2048], P('dp', 'tensor')
- grad_value: float32 [2304, 2048], P('dp', 'tensor')
- grad_pre_gain: float32 [2304], replicated
All inputs are finite; a program needn't handle non-finite values.
Results may differ from a plain program's by a relative error of at most 0.019.
The roundings to bfloat16 on the way count: a program that leaves them out, or rounds other values in their place, can miss the bound.
Values may be sent and summed in bfloat16 or wider, within the bound.
No kernel may reach another device: no remote copies, remote signals or barrier semaphores. Data moves between devices by JAX's collectives and lax.ppermute only.
A program may use at most 192 MiB of HBM per device.

v0:
```python
import functools
import jax
import jax.numpy as jnp
from jax import lax
from jax.sharding import Mesh
from jax.sharding import PartitionSpec as P

HEAD_SIZE = 128
SEQ_LEN = 64
TENSOR = ("tensor_0", "tensor_1")
DP = ("dp_0", "dp_1", "dp_2")
DP_TENSOR = ("dp_0", "dp_1", "dp_2", "tensor_0", "tensor_1")
EPS = 1e-06
CAP = 50.0
BASE = 10000.0
query_scalar = 144.0


def in_one_piece(arrays, axis, dim, along):
    widths = [a.shape[along] for a in arrays]
    both = jnp.concatenate(arrays, axis=along)
    result = lax.all_gather(both, axis, axis=dim, tiled=True)
    return tuple(jnp.split(result, [sum(widths[:k]) for k in range(1, len(widths))], axis=along))


def split_up(value, dim, devices):
    before, after = (value.shape[:dim], value.shape[dim + 1 :])
    return jnp.moveaxis(value.reshape(*before, devices, -1, *after), dim, 0)


def sum_at_owner(value, axis, dim):
    devices = lax.axis_size(axis)
    parts = lax.all_to_all(split_up(value, dim, devices), axis, 0, 0, tiled=True)
    return jnp.sum(parts.astype(jnp.float32), axis=0)


def one_axis_at_a_time(value, axes):
    return functools.reduce(lax.psum, axes, value)


def rotary_tables(segment_length, half):
    places = jnp.arange(segment_length, dtype=jnp.float32)[:, None]
    freqs = BASE ** (-jnp.arange(half, dtype=jnp.float32) / half)
    angles = places * freqs[None, :]
    return (jnp.cos(angles)[:, None, :], jnp.sin(angles)[:, None, :])


def rotate(values, cosine_table, sine_table):
    half = values.shape[-1] // 2
    first, second = (values[..., :half], values[..., half:])
    return jnp.concatenate(
        [first * cosine_table - second * sine_table, second * cosine_table + first * sine_table], -1
    )


def inverse_rotation(values, cosine_table, sine_table):
    half = values.shape[-1] // 2
    first, second = (values[..., :half], values[..., half:])
    return jnp.concatenate(
        [first * cosine_table + second * sine_table, second * cosine_table - first * sine_table], -1
    )


def attend_forward(query, key, value):
    repeat = query.shape[1] // key.shape[1]
    keys = jnp.repeat(key, repeat, axis=1)
    values = jnp.repeat(value, repeat, axis=1)
    factor = query_scalar ** (-0.5)
    raw = jnp.einsum("qhd,khd->hqk", query, keys, preferred_element_type=jnp.float32) * factor
    bent = jnp.tanh(raw / CAP)
    capped = CAP * bent
    segment_length = query.shape[0]
    causal = jnp.arange(segment_length)[None, :] <= jnp.arange(segment_length)[:, None]
    raised = jnp.where(causal[None], jnp.exp(capped), 0.0)
    weights = raised / jnp.sum(raised, -1, keepdims=True)
    probs = weights.astype(jnp.bfloat16)
    attended = jnp.einsum("hqk,khd->qhd", probs, values, preferred_element_type=jnp.float32).astype(
        jnp.bfloat16
    )
    return (attended, weights, probs, bent)


def attend_backward(d_attended, query, key, value, weights, probs, bent):
    repeat = query.shape[1] // key.shape[1]
    keys = jnp.repeat(key, repeat, axis=1)
    values = jnp.repeat(value, repeat, axis=1)
    factor = query_scalar ** (-0.5)
    d_probs = jnp.einsum("qhd,khd->hqk", d_attended, values, preferred_element_type=jnp.float32)
    d_capped = weights * (d_probs - jnp.sum(weights * d_probs, -1, keepdims=True))
    d_scores = (d_capped * (1.0 - bent * bent) * factor).astype(jnp.bfloat16)
    query_back = jnp.einsum("hqk,khd->qhd", d_scores, keys, preferred_element_type=jnp.float32)
    key_heads = jnp.einsum("hqk,qhd->khd", d_scores, query, preferred_element_type=jnp.float32)
    value_heads = jnp.einsum("hqk,qhd->khd", probs, d_attended, preferred_element_type=jnp.float32)
    segment_length, heads, width = query.shape
    key_rotated_back = key_heads.reshape(segment_length, heads // repeat, repeat, width).sum(2)
    value_returned = value_heads.reshape(segment_length, heads // repeat, repeat, width).sum(2)
    return (query_back, key_rotated_back, value_returned)


def segment_pass(query, key, value, d_attended):
    attended, weights, probs, bent = attend_forward(query, key, value)
    query_back, key_rotated_back, value_returned = attend_backward(
        d_attended, query, key, value, weights, probs, bent
    )
    return (attended, query_back, key_rotated_back, value_returned)


def per_device(tokens, cotangent, pre_gain, w_query, key_weight, value_weight):
    contract_first = (((0,), (0,)), ((), ()))
    contract_last = (((1,), (1,)), ((), ()))
    rows_f = tokens.astype(jnp.float32)
    inv_one = lax.rsqrt(jnp.mean(rows_f * rows_f, -1, keepdims=True) + EPS)
    unit_one = rows_f * inv_one
    normed_input = (unit_one * pre_gain).astype(jnp.bfloat16)
    gathered = lax.all_gather(normed_input, TENSOR, axis=0, tiled=True)
    segment_length = gathered.shape[0]
    token_span = SEQ_LEN
    pieces_count = segment_length // token_span
    heads_query = w_query.shape[1] // HEAD_SIZE
    heads_key = key_weight.shape[1] // HEAD_SIZE
    pieces = in_one_piece((w_query, key_weight, value_weight), DP, 0, 1)
    query_raw, key_unrotated, value_projected = tuple(
        (jnp.dot(gathered, piece, preferred_element_type=jnp.float32) for piece in pieces)
    )
    cosine_table, sine_table = rotary_tables(token_span, HEAD_SIZE // 2)
    query = rotate(
        query_raw.reshape(pieces_count, token_span, heads_query, HEAD_SIZE),
        cosine_table,
        sine_table,
    ).astype(jnp.bfloat16)
    key = rotate(
        key_unrotated.reshape(pieces_count, token_span, heads_key, HEAD_SIZE),
        cosine_table,
        sine_table,
    ).astype(jnp.bfloat16)
    value = value_projected.reshape(pieces_count, token_span, heads_key, HEAD_SIZE).astype(
        jnp.bfloat16
    )
    d_attended = cotangent.reshape(pieces_count, token_span, heads_query, HEAD_SIZE)
    attended, query_back, key_rotated_back, value_returned = jax.vmap(segment_pass)(
        query, key, value, d_attended
    )
    attended_flat = attended.reshape(segment_length, heads_query * HEAD_SIZE)
    d_query = (
        inverse_rotation(query_back, cosine_table, sine_table)
        .astype(jnp.bfloat16)
        .reshape(segment_length, heads_query * HEAD_SIZE)
    )
    key_gradient = (
        inverse_rotation(key_rotated_back, cosine_table, sine_table)
        .astype(jnp.bfloat16)
        .reshape(segment_length, heads_key * HEAD_SIZE)
    )
    value_gradient = value_returned.astype(jnp.bfloat16).reshape(
        segment_length, heads_key * HEAD_SIZE
    )
    back_query, back_key, back_value = in_one_piece((w_query, key_weight, value_weight), DP, 0, 1)
    joined = jnp.concatenate([d_query, key_gradient, value_gradient], 1)
    block = gathered
    grads = sum_at_owner(
        lax.dot_general(block, joined, contract_first, preferred_element_type=jnp.float32).astype(
            jnp.bfloat16
        ),
        DP,
        0,
    )
    width_query = w_query.shape[1]
    width_key = key_weight.shape[1]
    grad_query = grads[:, :width_query]
    grad_key = grads[:, width_query : width_query + width_key]
    grad_value = grads[:, width_query + width_key :]
    total = jnp.zeros((tokens.shape[0] * lax.axis_size(TENSOR), gathered.shape[1]), jnp.float32)
    for grad_part, weight in (
        (d_query, back_query),
        (key_gradient, back_key),
        (value_gradient, back_value),
    ):
        block = grad_part
        total = total + lax.dot_general(
            block, weight, contract_last, preferred_element_type=jnp.float32
        )
    d_normed = lax.psum_scatter(
        total.astype(jnp.bfloat16), TENSOR, scatter_dimension=0, tiled=True
    ).astype(jnp.float32)
    pre_part = jnp.sum(d_normed * unit_one, 0)
    scaled_in = d_normed * pre_gain
    grad_tokens = (
        inv_one * (scaled_in - unit_one * jnp.mean(scaled_in * unit_one, -1, keepdims=True))
    ).astype(jnp.bfloat16)
    grad_pre = one_axis_at_a_time(pre_part, DP_TENSOR)
    return (attended_flat, grad_tokens, grad_query, grad_key, grad_value, grad_pre)


def solution(mesh):
    torus = Mesh(
        mesh.devices.reshape(4, 2, 2, 2, 8), ("dp_0", "dp_1", "dp_2", "tensor_0", "tensor_1")
    )
    in_specs = (P(DP_TENSOR, None), P(DP, TENSOR), P(), P(DP, TENSOR), P(DP, TENSOR), P(DP, TENSOR))
    out_specs = (
        P(DP, TENSOR),
        P(DP_TENSOR, None),
        P(DP, TENSOR),
        P(DP, TENSOR),
        P(DP, TENSOR),
        P(),
    )
    return jax.shard_map(
        per_device, mesh=torus, in_specs=in_specs, out_specs=out_specs, check_vma=False
    )
```

profile of v0, /device:TPU:4, one launch (start us, length us, event | category | flops | bytes accessed | tf_op | source)
XLA Modules:
  0.0 471.2 jit_solution(14125155676329583121)
XLA Ops:
  7.2 1.7 pad_maximum_fusion.5
  9.0 1.3 fusion.24
  10.3 2.1 fusion.22
  12.9 52.2 %all-gather.5.cloned.1.call-done = bf16[2304,512]{1,0:T(8,128)(2,1)} async-done(((bf16[144,512]{1,0:T(8,128)(2,1)}), bf16[2304,512]{1,0:T(8,128)(2,1)}) %all-gather.5.cloned.1.call-update) | async-done | bytes 2359312 | tf_op jit(solution)/shard_map/all_gather | solution.py:22
  65.1 114.8 %all-gather.3.cloned.1.call-done = bf16[2048,2304]{1,0:T(8,128)(2,1)} async-done(((bf16[128,2304]{1,0:T(8,128)(2,1)}), bf16[2048,2304]{1,0:T(8,128)(2,1)}) %all-gather.3.cloned.1.call-update) | async-done | bytes 9437200 | tf_op jit(solution)/shard_map/all_gather | solution.py:115
  179.9 7.9 %fusion.28 = f32[2048,256]{1,0:T(8,128)} fusion(bf16[2048,2304]{1,0:T(8,128)(2,1)} %all-gather.3.cloned.1.call-done, bf16[2304,512]{1,0:T(8,128)(2,1)} %all-gather.5.cloned.1.call-done), kind=kOutput, calls=%fused_computation.56 | convolution fusion | flops 2415919104 | bytes 12713984 | tf_op jit(solution)/shard_map/dot_general | solution.py:123
  187.8 2.3 reshape.131
  190.1 2.4 fusion.72
  192.6 6.3 %fusion.48 = f32[2048,128]{1,0:T(8,128)S(1)} fusion(bf16[2048,2304]{1,0:T(8,128)(2,1)} %all-gather.3.cloned.1.call-done, bf16[2304,512]{1,0:T(8,128)(2,1)S(1)} %copy-done.2), kind=kOutput, calls=%fused_computation.77 | convolution fusion | flops 1207959552 | bytes 11075584 | tf_op jit(solution)/shard_map/dot_general | solution.py:123
  199.7 2.7 convolution_convert_fusion.1
  204.0 2.6 fusion.13
  206.6 6.2 %convolution_bitcast_fusion.2 = f32[32,64,1,128]{3,1,0,2:T(8,128)} fusion(f32[32,2,64,64]{3,2,1,0:T(8,128)S(1)} %fusion.32, f32[32,2,64,64]{2,3,1,0:T(8,128)} %get-tuple-element.23, bf16[32,64,2,64]{3,1,2,0:T(8,128)(2,1)} %copy-done.10, bf16[32,64,2,64]{3,1,2,0:T(8,128)(2,1)} %copy-done.9, f32[32,2,64]{2,1,0:T(2,128)S(1)} %get-tuple-element.22, ...), kind=kOutput, calls=%fused_computation.38 | convolution fusion | flops 73404480 | bytes 4214784 | tf_op jit(solution)/shard_map/vmap(hqk,qhd->khd)/dot_general | solution.py:92
  212.8 6.3 %convolution_bitcast_fusion = f32[32,64,2,128]{3,1,2,0:T(8,128)S(1)} fusion(f32[32,2,64,64]{3,2,1,0:T(8,128)} %copy-done.8, f32[32,2,64,64]{2,3,1,0:T(8,128)} %get-tuple-element.23, bf16[32,64,128]{2,1,0:T(8,128)(2,1)} %copy-done.15, f32[32,2,64]{2,1,0:T(2,128)S(1)} %get-tuple-element.22, pred[64,64]{0,1:T(8,128)(4,1)S(1)} %iota_compare_fusion), kind=kOutput, calls=%fused_computation.24 | convolution fusion | flops 71307328 | bytes 4739072 | tf_op jit(solution)/shard_map/vmap(hqk,khd->qhd)/dot_general | solution.py:91
  219.1 3.2 fusion.19
  224.7 1.1 copy.24
  226.1 7.9 %fusion.26 = f32[2048,2304]{1,0:T(8,128)} fusion(bf16[2304,512]{1,0:T(8,128)(2,1)S(1)} %copy-done.3, bf16[256,8,2,128]{3,2,1,0:T(2,128)(2,1)S(1)} %bitcast.61), kind=kOutput, calls=%fused_computation.54 | convolution fusion | flops 2415919104 | bytes 21102592 | tf_op jit(solution)/shard_map/dot_general | solution.py:179
  234.1 7.9 %fusion.36 = f32[2048,2304]{1,0:T(8,128)} fusion(bf16[2048,64]{1,0:T(8,128)(2,1)S(1)} %bitcast.68, bf16[2048,64]{1,0:T(8,128)(2,1)S(1)} %bitcast.66, bf16[2304,512]{1,0:T(8,128)(2,1)S(1)} %copy-done.3), kind=kOutput, calls=%fused_computation.65 | convolution fusion | flops 1209008128 | bytes 20512768 | tf_op jit(solution)/shard_map/dot_general | solution.py:179
  242.0 17.2 %add_convert_fusion = bf16[2048,2304]{1,0:T(8,128)(2,1)} fusion(f32[2048,2304]{1,0:T(8,128)} %fusion.26, f32[2048,2304]{1,0:T(8,128)} %fusion.36, bf16[2048,128]{1,0:T(8,128)(2,1)} %bitcast.72, bf16[2304,512]{1,0:T(8,128)(2,1)S(1)} %copy-done.3), kind=kOutput, calls=%fused_computation.1 | convolution fusion | flops 1222115328 | bytes 48300032 | tf_op jit(solution)/shard_map/dot_general | solution.py:179
  259.4 0.9 copy-done.5
  260.6 11.8 %convolution_convert_fusion = bf16[2304,512]{1,0:T(8,128)(2,1)} fusion(bf16[2048,2304]{1,0:T(8,128)(2,1)} %all-gather.3.cloned.1.call-done, bf16[2048,128]{1,0:T(8,128)(2,1)S(1)} %bitcast.73, bf16[2048,64]{1,0:T(8,128)(2,1)S(1)} %bitcast.69, bf16[2048,64]{1,0:T(8,128)(2,1)S(1)} %bitcast.67, bf16[2048,256]{1,0:T(8,128)(2,1)S(1)} %bitcast.71), kind=kOutput, calls=%fused_computation.3 | convolution fusion | flops 4841406464 | bytes 13893632 | tf_op jit(solution)/shard_map/dot_general | solution.py:161
  272.4 7.4 %all-to-all-start = ((bf16[16,144,512]{2,1,0:T(8,128)(2,1)}), bf16[16,144,512]{2,1,0:T(8,128)(2,1)S(1)}, u32[]{:S(2)}, u32[]{:S(2)}) async-start(bf16[16,144,512]{2,1,0:T(8,128)(2,1)} %bitcast.65), calls=%async_computation.1 | async-start | bytes 4718592 | tf_op jit(solution)/shard_map/all_to_all | solution.py:33
  279.8 2.5 fusion.18
  282.3 1.1 copy.21
  283.4 1.1 copy.46
  284.5 108.6 %all-to-all-done = bf16[16,144,512]{2,1,0:T(8,128)(2,1)S(1)} async-done(((bf16[16,144,512]{2,1,0:T(8,128)(2,1)}), bf16[16,144,512]{2,1,0:T(8,128)(2,1)S(1)}, u32[]{:S(2)}, u32[]{:S(2)}) %all-to-all-start) | async-done | bytes 2359328 | tf_op jit(solution)/shard_map/all_to_all | solution.py:33
  394.8 1.5 fusion.25
  396.3 16.0 %psum.35 = f32[2304]{0:T(1024)S(1)} all-reduce(f32[2304]{0:T(1024)S(1)} %get-tuple-element.6), channel_id=1, replica_groups=mesh['dp_0'=4,'dp_1'=2,'dp_2'=2,'tensor_0'=2,'tensor_1'=8] {'dp_0'}, use_global_device_ids=true, to_apply=%region_7.8 | all-reduce | flops 2304 | bytes 18432 | tf_op jit(solution)/shard_map/psum | solution.py:38
  412.3 11.9 %psum.36 = f32[2304]{0:T(1024)S(1)} all-reduce(f32[2304]{0:T(1024)S(1)} %psum.35), channel_id=1, replica_groups=mesh['dp_0'=4,'dp_1'=2,'dp_2'=2,'tensor_0'=2,'tensor_1'=8] {'dp_1'}, use_global_device_ids=true, to_apply=%region_8.9 | all-reduce | flops 2304 | bytes 18432 | tf_op jit(solution)/shard_map/psum | solution.py:38
  424.2 3.3 psum.37
  427.5 7.7 %psum.38 = f32[2304]{0:T(1024)S(1)} all-reduce(f32[2304]{0:T(1024)S(1)} %psum.37), channel_id=1, replica_groups=mesh['dp_0'=4,'dp_1'=2,'dp_2'=2,'tensor_0'=2,'tensor_1'=8] {'tensor_0'}, use_global_device_ids=true, to_apply=%region_10.11 | all-reduce | flops 2304 | bytes 18432 | tf_op jit(solution)/shard_map/psum | solution.py:38
  435.2 27.2 %psum.39 = f32[2304]{0:T(1024)} all-reduce(f32[2304]{0:T(1024)S(1)} %psum.38), channel_id=1, replica_groups=mesh['dp_0'=4,'dp_1'=2,'dp_2'=2,'tensor_0'=2,'tensor_1'=8] {'tensor_1'}, use_global_device_ids=true, to_apply=%region_11.12 | all-reduce | flops 2304 | bytes 18432 | tf_op jit(solution)/shard_map/psum | solution.py:38
  462.4 2.3 fusion.21
  (64 shorter events, 7.6 us)
Async XLA Ops:
  7.2 5.2 %copy-start.11 = (bf16[2048,256]{1,0:T(8,128)(2,1)S(1)}, bf16[2048,256]{1,0:T(8,128)(2,1)}, u32[]{:S(2)}) copy-start(bf16[2048,256]{1,0:T(8,128)(2,1)} %param.7) | copy-start | bytes 3145732
  7.2 57.9 %all-gather.5.cloned.1.call-start = ((), (), s32[]{:S(2)}) async-start(), calls=%async_computation.3 | async-start | bytes 2506752 | tf_op jit(solution)/shard_map/all_gather | solution.py:22
  8.9 171.0 %all-gather.3.cloned.1.call-start = ((), (), s32[]{:S(2)}) async-start(), calls=%async_computation.2 | async-start | bytes 10027008 | tf_op jit(solution)/shard_map/all_gather | solution.py:115
  12.4 382.4 %reduce-scatter.2.cloned.1.call-start = ((), (), s32[]{:S(2)}) async-start(), calls=%async_computation.4 | async-start | bytes 10027008 | tf_op jit(solution)/shard_map/reduce_scatter | solution.py:182
  190.1 2.5 copy-start.2
  190.1 9.6 %slice-start = ((s8[9437184]{0:T(1024)(128)(4,1)}), s8[4194304]{0:T(1024)(128)(4,1)S(1)}, s32[]{:S(2)}) async-start(s8[9437184]{0:T(1024)(128)(4,1)} %bitcast.76), calls=%async_computation.5 | async-start | bytes 8388608
  192.6 7.1 %slice-start.1 = ((s8[9437184]{0:T(1024)(128)(4,1)}), s8[4194304]{0:T(1024)(128)(4,1)S(1)}, s32[]{:S(2)}) async-start(s8[9437184]{0:T(1024)(128)(4,1)} %bitcast.76), calls=%async_computation.6 | async-start | bytes 8388608
  192.6 7.1 %slice-start.2 = ((s8[9437184]{0:T(1024)(128)(4,1)}), s8[1048576]{0:T(1024)(128)(4,1)S(1)}, s32[]{:S(2)}) async-start(s8[9437184]{0:T(1024)(128)(4,1)} %bitcast.76), calls=%async_computation.7 | async-start | bytes 2097152
  199.7 4.2 copy-start.15
  202.4 0.8 copy-start.13
  203.1 3.5 copy-start.8
  203.9 2.7 copy-start.9
  203.9 2.7 copy-start.10
  222.4 1.2 copy-start.1
  224.0 10.0 %copy-start.4 = (bf16[32,64,1,64]{3,1,0,2:T(8,128)(2,1)}, bf16[32,64,1,64]{3,1,0,2:T(8,128)(2,1)S(1)}, u32[]{:S(2)}) copy-start(bf16[32,64,1,64]{3,1,0,2:T(8,128)(2,1)S(1)} %get-tuple-element.14) | copy-start | bytes 786436
  224.0 10.0 %copy-start.6 = (bf16[32,64,1,64]{3,1,0,2:T(8,128)(2,1)}, bf16[32,64,1,64]{3,1,0,2:T(8,128)(2,1)S(1)}, u32[]{:S(2)}) copy-start(bf16[32,64,1,64]{3,1,0,2:T(8,128)(2,1)S(1)} %get-tuple-element.15) | copy-start | bytes 786436
  224.1 2.0 copy-start.3
  259.2 1.0 copy-start.5
  259.2 1.2 copy-start.7
  259.2 1.3 copy-start.12
  272.4 7.4 %copy-start.14 = (bf16[2048,128]{1,0:T(8,128)(2,1)S(1)}, bf16[2048,128]{1,0:T(8,128)(2,1)}, u32[]{:S(2)}) copy-start(bf16[2048,128]{1,0:T(8,128)(2,1)} %copy-done.13) | copy-start | bytes 1572868
  272.4 120.7 %all-to-all-start = ((bf16[16,144,512]{2,1,0:T(8,128)(2,1)}), bf16[16,144,512]{2,1,0:T(8,128)(2,1)S(1)}, u32[]{:S(2)}, u32[]{:S(2)}) async-start(bf16[16,144,512]{2,1,0:T(8,128)(2,1)} %bitcast.65), calls=%async_computation.1 | async-start | bytes 4718592 | tf_op jit(solution)/shard_map/all_to_all | solution.py:33
  284.5 110.3 %copy-start = (bf16[128,2304]{1,0:T(8,128)(2,1)S(1)}, bf16[128,2304]{1,0:T(8,128)(2,1)}, u32[]{:S(2)}) copy-start(bf16[128,2304]{1,0:T(8,128)(2,1)} %param.6) | copy-start | bytes 1769476
  284.5 110.3 %copy-start.16 = (f32[2304]{0:T(1024)S(1)}, f32[2304]{0:T(1024)}, u32[]{:S(2)}) copy-start(f32[2304]{0:T(1024)} %param.8) | copy-start | bytes 27652
Sparse Core Ops, SparseCore 0:
  11.3 53.7 all-gather.4
  67.4 112.4 all-gather.2
  259.3 109.5 reduce-scatter.1
where the time goes:
time: 472 us; the launch traced here: 471 us
  waiting for transfers between devices  276 us (58%)
  matrix products  83.3 us (18%)
  blocking collectives  66.1 us (14%)
  between operations  14.1 us (3%)
  other arithmetic  12.6 us (3%)
  local copies, waits for them, and re-layouts  11.9 us (3%)
  starting transfers between devices  7.51 us (2%)
    all_gather x1, waiting for transfers between devices, per_device(): gathered = lax.all_gather(normed_input, TENSOR, axis=0, tiled=True)  115 us
    all_to_all x1, waiting for transfers between devices, sum_at_owner(): lax.all_to_all(split_up(value, dim, devices), axis, 0, 0, tiled=True)  109 us
    psum x5, blocking collectives, one_axis_at_a_time(): return functools.reduce(lax.psum, axes, value)  66.1 us
    all_gather x1, waiting for transfers between devices, in_one_piece(): result = lax.all_gather(both, axis, axis=dim, tiled=True)  52.2 us
    dot_general x3, matrix products, per_device(): lax.dot_general(block, weight, contract_last, preferred_element_type=jnp....  33.1 us
    dot_general x3, matrix products, per_device(): jnp.dot(gathered, piece, preferred_element_type=jnp.float32)  16.9 us
    dot_general x1, matrix products, per_device(): lax.dot_general(block, joined, contract_first, preferred_element_type=jnp...  11.8 us
  transfers between devices with their start and end apart: 4, of which 3 were waited for; matrix products, arithmetic and copies ran while one was open for 5% of the time, Pallas kernels for 0%

commit v1 on v0

--- a/solution.py
+++ b/solution.py
@@ -112,7 +112,8 @@
     inv_one = lax.rsqrt(jnp.mean(rows_f * rows_f, -1, keepdims=True) + EPS)
     unit_one = rows_f * inv_one
     normed_input = (unit_one * pre_gain).astype(jnp.bfloat16)
-    gathered = lax.all_gather(normed_input, TENSOR, axis=0, tiled=True)
+    outgoing = jnp.stack([normed_input] * lax.axis_size(TENSOR))
+    gathered = jnp.concatenate(lax.all_to_all(outgoing, TENSOR, 0, 0), axis=0)
     segment_length = gathered.shape[0]
     token_span = SEQ_LEN
     pieces_count = segment_length // token_span

time: 472 us -> 530 us (1.12)
  waiting for transfers between devices: 276 us -> 322 us
  starting transfers between devices: 7.51 us -> 17.1 us
    all_to_all x0 -> x1, waiting for transfers between devices: none -> 140 us  [per_device(): gathered = jnp.concatenate(lax.all_to_all(outgoing, TENSOR, 0, 0), axis=0)]
    all_gather x1 -> x0, waiting for transfers between devices: 115 us -> none  [per_device(): gathered = lax.all_gather(normed_input, TENSOR, axis=0, tiled=True)]
    all_gather x1, waiting for transfers between devices: 52.2 us -> 65.9 us  [in_one_piece(): result = lax.all_gather(both, axis, axis=dim, tiled=True)]
    all_to_all x0 -> x1, starting transfers between devices: none -> 9.39 us  [per_device(): gathered = jnp.concatenate(lax.all_to_all(outgoing, TENSOR, 0, 0), axis=0)]
    all_to_all x1, waiting for transfers between devices: 109 us -> 116 us  [sum_at_owner(): lax.all_to_all(split_up(value, dim, devices), axis, 0, 0, tiled=True)]
  transfers between devices with their start and end apart: 4 -> 4, of which waited for: 3 -> 3; matrix products, arithmetic and copies ran while one was open for 5% -> 4% of each run, Pallas kernels for 0% -> 0%
where the time goes in v1:
time: 530 us; the launch traced here: 529 us
  waiting for transfers between devices  322 us (61%)
  matrix products  83.4 us (16%)
  blocking collectives  65.9 us (12%)
  starting transfers between devices  17.1 us (3%)
  local copies, waits for them, and re-layouts  15.4 us (3%)
  between operations  14.4 us (3%)
  other arithmetic  10.8 us (2%)
    all_to_all x1, waiting for transfers between devices, per_device(): gathered = jnp.concatenate(lax.all_to_all(outgoing, TENSOR, 0, 0), axis=0)  140 us
    all_to_all x1, waiting for transfers between devices, sum_at_owner(): lax.all_to_all(split_up(value, dim, devices), axis, 0, 0, tiled=True)  116 us
    all_gather x1, waiting for transfers between devices, in_one_piece(): result = lax.all_gather(both, axis, axis=dim, tiled=True)  65.9 us
    psum x5, blocking collectives, one_axis_at_a_time(): return functools.reduce(lax.psum, axes, value)  65.9 us
    dot_general x3, matrix products, per_device(): lax.dot_general(block, weight, contract_last, preferred_element_type=jnp....  33.1 us
    dot_general x3, matrix products, per_device(): jnp.dot(gathered, piece, preferred_element_type=jnp.float32)  17.4 us
    dot_general x1, matrix products, per_device(): lax.dot_general(block, joined, contract_first, preferred_element_type=jnp...  11.8 us
  transfers between devices with their start and end apart: 4, of which 3 were waited for; matrix products, arithmetic and copies ran while one was open for 4% of the time, Pallas kernels for 0%

profile of v1, /device:TPU:4, one launch (start us, length us, event | category | flops | bytes accessed | tf_op | source)
XLA Modules:
  0.0 529.1 jit_solution(11373758624215268763)
XLA Ops:
  7.2 1.3 fusion.24
  8.4 1.3 fusion.22
  9.7 4.5 stack.2
  14.3 9.4 %all-to-all-start = ((bf16[16,128,2304]{2,1,0:T(8,128)(2,1)}), bf16[16,128,2304]{2,1,0:T(8,128)(2,1)}, u32[]{:S(2)}, u32[]{:S(2)}) async-start(bf16[16,128,2304]{2,1,0:T(8,128)(2,1)} %stack.2), calls=%async_computation | async-start | bytes 18874368 | tf_op jit(solution)/shard_map/all_to_all | solution.py:116
  25.0 65.9 %all-gather.2.cloned.1.call-done = bf16[2304,512]{1,0:T(8,128)(2,1)} async-done(((bf16[144,512]{1,0:T(8,128)(2,1)}), bf16[2304,512]{1,0:T(8,128)(2,1)}) %all-gather.2.cloned.1.call-update) | async-done | bytes 2359312 | tf_op jit(solution)/shard_map/all_gather | solution.py:22
  90.9 1.3 slice_bitcast_fusion
  92.3 1.6 copy.29
  93.8 139.9 %all-to-all-done = bf16[16,128,2304]{2,1,0:T(8,128)(2,1)} async-done(((bf16[16,128,2304]{2,1,0:T(8,128)(2,1)}), bf16[16,128,2304]{2,1,0:T(8,128)(2,1)}, u32[]{:S(2)}, u32[]{:S(2)}) %all-to-all-start) | async-done | bytes 9437216 | tf_op jit(solution)/shard_map/all_to_all | solution.py:116
  233.7 5.7 %fusion.72 = f32[32,64,2,128]{3,1,2,0:T(8,128)S(1)} fusion(bf16[32,64,2304,1]{2,1,3,0:T(8,128)(2,1)} %bitcast.3, bf16[2,128,2304,1]{2,1,0,3:T(8,128)(2,1)} %bitcast.87), kind=kOutput, calls=%fused_computation.103 | convolution fusion | flops 2415919104 | bytes 12713984 | tf_op jit(solution)/shard_map/dot_general | solution.py:124
  241.0 5.2 convolution_bitcast_fusion.3
  247.0 6.5 %convolution_convert_fusion.2 = bf16[32,64,128]{2,1,0:T(8,128)(2,1)S(1)} fusion(bf16[32,64,2304]{2,1,0:T(8,128)(2,1)} %bitcast, bf16[2304,512]{1,0:T(8,128)(2,1)S(1)} %copy-done.1), kind=kOutput, calls=%fused_computation.40 | convolution fusion | flops 1208221696 | bytes 10551296 | tf_op jit(solution)/shard_map/dot_general | solution.py:124
  254.2 2.6 fusion.13
  256.9 6.2 %convolution_bitcast_fusion.2 = f32[32,64,1,128]{3,1,0,2:T(8,128)} fusion(f32[32,2,64,64]{3,2,1,0:T(8,128)S(1)} %fusion.30, f32[32,2,64,64]{2,3,1,0:T(8,128)} %get-tuple-element.21, bf16[32,64,2,64]{3,1,2,0:T(8,128)(2,1)} %copy-done.10, bf16[32,64,2,64]{3,1,2,0:T(8,128)(2,1)} %copy-done.9, f32[32,2,64]{2,1,0:T(2,128)S(1)} %get-tuple-element.20, ...), kind=kOutput, calls=%fused_computation.37 | convolution fusion | flops 73404480 | bytes 4214784 | tf_op jit(solution)/shard_map/vmap(hqk,qhd->khd)/dot_general | solution.py:92
  263.1 5.9 %convolution_bitcast_fusion = f32[32,64,2,128]{3,1,2,0:T(8,128)S(1)} fusion(f32[32,2,64,64]{3,2,1,0:T(8,128)} %copy-done.8, f32[32,2,64,64]{2,3,1,0:T(8,128)} %get-tuple-element.21, bf16[32,64,128]{2,1,0:T(8,128)(2,1)} %copy-done.15, f32[32,2,64]{2,1,0:T(2,128)S(1)} %get-tuple-element.20, pred[64,64]{0,1:T(8,128)(4,1)S(1)} %iota_compare_fusion), kind=kOutput, calls=%fused_computation.23 | convolution fusion | flops 71307328 | bytes 4739072 | tf_op jit(solution)/shard_map/vmap(hqk,khd->qhd)/dot_general | solution.py:91
  269.1 3.2 fusion.19
  274.6 1.1 copy.22
  276.0 8.0 %fusion.26 = f32[2048,2304]{1,0:T(8,128)} fusion(bf16[2304,512]{1,0:T(8,128)(2,1)S(1)} %copy-done.2, bf16[256,8,2,128]{3,2,1,0:T(2,128)(2,1)S(1)} %bitcast.79), kind=kOutput, calls=%fused_computation.55 | convolution fusion | flops 2415919104 | bytes 21102592 | tf_op jit(solution)/shard_map/dot_general | solution.py:180
  284.0 7.9 %fusion.36 = f32[2048,2304]{1,0:T(8,128)} fusion(bf16[2048,64]{1,0:T(8,128)(2,1)S(1)} %bitcast.85, bf16[2048,64]{1,0:T(8,128)(2,1)S(1)} %bitcast.83, bf16[2304,512]{1,0:T(8,128)(2,1)S(1)} %copy-done.2), kind=kOutput, calls=%fused_computation.67 | convolution fusion | flops 1209008128 | bytes 20512768 | tf_op jit(solution)/shard_map/dot_general | solution.py:180
  291.9 17.2 %add_convert_fusion = bf16[2048,2304]{1,0:T(8,128)(2,1)} fusion(f32[2048,2304]{1,0:T(8,128)} %fusion.26, f32[2048,2304]{1,0:T(8,128)} %fusion.36, bf16[2048,128]{1,0:T(8,128)(2,1)} %bitcast.90, bf16[2304,512]{1,0:T(8,128)(2,1)S(1)} %copy-done.2), kind=kOutput, calls=%fused_computation.1 | convolution fusion | flops 1222115328 | bytes 48300032 | tf_op jit(solution)/shard_map/dot_general | solution.py:180
  310.5 11.8 %convolution_convert_fusion = bf16[2304,512]{1,0:T(8,128)(2,1)} fusion(bf16[2048,2304]{1,0:T(8,128)(2,1)} %bitcast.22, bf16[2048,128]{1,0:T(8,128)(2,1)S(1)} %bitcast.91, bf16[2048,64]{1,0:T(8,128)(2,1)S(1)} %bitcast.86, bf16[2048,64]{1,0:T(8,128)(2,1)S(1)} %bitcast.84, bf16[2048,256]{1,0:T(8,128)(2,1)S(1)} %bitcast.89), kind=kOutput, calls=%fused_computation.3 | convolution fusion | flops 4841406464 | bytes 13893632 | tf_op jit(solution)/shard_map/dot_general | solution.py:162
  322.4 7.6 %all-to-all-start.1 = ((bf16[16,144,512]{2,1,0:T(8,128)(2,1)}), bf16[16,144,512]{2,1,0:T(8,128)(2,1)S(1)}, u32[]{:S(2)}, u32[]{:S(2)}) async-start(bf16[16,144,512]{2,1,0:T(8,128)(2,1)} %bitcast.82), calls=%async_computation.2 | async-start | bytes 4718592 | tf_op jit(solution)/shard_map/all_to_all | solution.py:33
  329.9 2.4 fusion.18
  332.4 1.1 copy.19
  333.5 1.1 copy.40
  334.6 116.3 %all-to-all-done.1 = bf16[16,144,512]{2,1,0:T(8,128)(2,1)S(1)} async-done(((bf16[16,144,512]{2,1,0:T(8,128)(2,1)}), bf16[16,144,512]{2,1,0:T(8,128)(2,1)S(1)}, u32[]{:S(2)}, u32[]{:S(2)}) %all-to-all-start.1) | async-done | bytes 2359328 | tf_op jit(solution)/shard_map/all_to_all | solution.py:33
  452.5 1.5 fusion.25
  454.1 16.0 %psum.35 = f32[2304]{0:T(1024)S(1)} all-reduce(f32[2304]{0:T(1024)S(1)} %get-tuple-element.6), channel_id=1, replica_groups=mesh['dp_0'=4,'dp_1'=2,'dp_2'=2,'tensor_0'=2,'tensor_1'=8] {'dp_0'}, use_global_device_ids=true, to_apply=%region_7.8 | all-reduce | flops 2304 | bytes 18432 | tf_op jit(solution)/shard_map/psum | solution.py:38
  470.0 11.9 %psum.36 = f32[2304]{0:T(1024)S(1)} all-reduce(f32[2304]{0:T(1024)S(1)} %psum.35), channel_id=1, replica_groups=mesh['dp_0'=4,'dp_1'=2,'dp_2'=2,'tensor_0'=2,'tensor_1'=8] {'dp_1'}, use_global_device_ids=true, to_apply=%region_8.9 | all-reduce | flops 2304 | bytes 18432 | tf_op jit(solution)/shard_map/psum | solution.py:38
  481.9 3.3 psum.37
  485.2 7.7 %psum.38 = f32[2304]{0:T(1024)S(1)} all-reduce(f32[2304]{0:T(1024)S(1)} %psum.37), channel_id=1, replica_groups=mesh['dp_0'=4,'dp_1'=2,'dp_2'=2,'tensor_0'=2,'tensor_1'=8] {'tensor_0'}, use_global_device_ids=true, to_apply=%region_10.11 | all-reduce | flops 2304 | bytes 18432 | tf_op jit(solution)/shard_map/psum | solution.py:38
  492.9 27.0 %psum.39 = f32[2304]{0:T(1024)} all-reduce(f32[2304]{0:T(1024)S(1)} %psum.38), channel_id=1, replica_groups=mesh['dp_0'=4,'dp_1'=2,'dp_2'=2,'tensor_0'=2,'tensor_1'=8] {'tensor_1'}, use_global_device_ids=true, to_apply=%region_11.12 | all-reduce | flops 2304 | bytes 18432 | tf_op jit(solution)/shard_map/psum | solution.py:38
  520.0 2.3 fusion.21
  (63 shorter events, 10.0 us)
Async XLA Ops:
  14.3 9.5 %copy-start.17 = (bf16[144,256]{1,0:T(8,128)(2,1)S(1)}, bf16[144,256]{1,0:T(8,128)(2,1)}, u32[]{:S(2)}) copy-start(bf16[144,256]{1,0:T(8,128)(2,1)} %param.9) | copy-start | bytes 221188
  14.3 9.5 %copy-start.18 = (bf16[144,128]{1,0:T(8,128)(2,1)S(1)}, bf16[144,128]{1,0:T(8,128)(2,1)}, u32[]{:S(2)}) copy-start(bf16[144,128]{1,0:T(8,128)(2,1)} %param.11) | copy-start | bytes 110596
  14.3 9.5 %copy-start.19 = (bf16[144,128]{1,0:T(8,128)(2,1)S(1)}, bf16[144,128]{1,0:T(8,128)(2,1)}, u32[]{:S(2)}) copy-start(bf16[144,128]{1,0:T(8,128)(2,1)} %param.10) | copy-start | bytes 110596
  14.3 10.2 %copy-start.11 = (bf16[2048,256]{1,0:T(8,128)(2,1)S(1)}, bf16[2048,256]{1,0:T(8,128)(2,1)}, u32[]{:S(2)}) copy-start(bf16[2048,256]{1,0:T(8,128)(2,1)} %param.7) | copy-start | bytes 3145732
  14.3 219.4 %all-to-all-start = ((bf16[16,128,2304]{2,1,0:T(8,128)(2,1)}), bf16[16,128,2304]{2,1,0:T(8,128)(2,1)}, u32[]{:S(2)}, u32[]{:S(2)}) async-start(bf16[16,128,2304]{2,1,0:T(8,128)(2,1)} %stack.2), calls=%async_computation | async-start | bytes 18874368 | tf_op jit(solution)/shard_map/all_to_all | solution.py:116
  23.7 67.2 %all-gather.2.cloned.1.call-start = ((), (), s32[]{:S(2)}) async-start(), calls=%async_computation.3 | async-start | bytes 2506752 | tf_op jit(solution)/shard_map/all_gather | solution.py:22
  24.4 428.1 %reduce-scatter.2.cloned.1.call-start = ((), (), s32[]{:S(2)}) async-start(), calls=%async_computation.4 | async-start | bytes 10027008 | tf_op jit(solution)/shard_map/reduce_scatter | solution.py:183
  239.4 1.7 copy-start.1
  240.1 14.1 %copy-start.9 = (bf16[32,64,2,64]{3,1,2,0:T(8,128)(2,1)}, bf16[32,64,2,64]{3,1,2,0:T(8,128)(2,1)S(1)}, u32[]{:S(2)}) copy-start(bf16[32,64,2,64]{3,1,2,0:T(8,128)(2,1)S(1)} %get-tuple-element.10) | copy-start | bytes 1572868
  240.1 14.1 %copy-start.10 = (bf16[32,64,2,64]{3,1,2,0:T(8,128)(2,1)}, bf16[32,64,2,64]{3,1,2,0:T(8,128)(2,1)S(1)}, u32[]{:S(2)}) copy-start(bf16[32,64,2,64]{3,1,2,0:T(8,128)(2,1)S(1)} %get-tuple-element.11) | copy-start | bytes 1572868
  247.0 7.2 %copy-start.15 = (bf16[32,64,128]{2,1,0:T(8,128)(2,1)}, bf16[32,64,128]{2,1,0:T(8,128)(2,1)S(1)}, u32[]{:S(2)}) copy-start(bf16[32,64,128]{2,1,0:T(8,128)(2,1)S(1)} %pad_maximum_fusion.2) | copy-start | bytes 1572868
  253.5 3.4 copy-start.13
  254.2 2.7 copy-start.8
  272.3 1.2 copy-start.3
  274.0 10.0 %copy-start.4 = (bf16[32,64,1,64]{3,1,0,2:T(8,128)(2,1)}, bf16[32,64,1,64]{3,1,0,2:T(8,128)(2,1)S(1)}, u32[]{:S(2)}) copy-start(bf16[32,64,1,64]{3,1,0,2:T(8,128)(2,1)S(1)} %get-tuple-element.12) | copy-start | bytes 786436
  274.0 10.0 %copy-start.6 = (bf16[32,64,1,64]{3,1,0,2:T(8,128)(2,1)}, bf16[32,64,1,64]{3,1,0,2:T(8,128)(2,1)S(1)}, u32[]{:S(2)}) copy-start(bf16[32,64,1,64]{3,1,0,2:T(8,128)(2,1)S(1)} %get-tuple-element.13) | copy-start | bytes 786436
  274.0 2.0 copy-start.2
  309.1 1.0 copy-start.5
  309.2 1.2 copy-start.7
  309.2 1.3 copy-start.12
  322.4 7.6 %copy-start.14 = (bf16[32,64,128]{2,1,0:T(8,128)(2,1)S(1)}, bf16[32,64,128]{2,1,0:T(8,128)(2,1)}, u32[]{:S(2)}) copy-start(bf16[32,64,128]{2,1,0:T(8,128)(2,1)} %copy-done.13) | copy-start | bytes 1572868
  322.4 128.5 %all-to-all-start.1 = ((bf16[16,144,512]{2,1,0:T(8,128)(2,1)}), bf16[16,144,512]{2,1,0:T(8,128)(2,1)S(1)}, u32[]{:S(2)}, u32[]{:S(2)}) async-start(bf16[16,144,512]{2,1,0:T(8,128)(2,1)} %bitcast.82), calls=%async_computation.2 | async-start | bytes 4718592 | tf_op jit(solution)/shard_map/all_to_all | solution.py:33
  334.6 117.9 %copy-start = (bf16[128,2304]{1,0:T(8,128)(2,1)S(1)}, bf16[128,2304]{1,0:T(8,128)(2,1)}, u32[]{:S(2)}) copy-start(bf16[128,2304]{1,0:T(8,128)(2,1)} %param.6) | copy-start | bytes 1769476
  334.6 117.9 %copy-start.16 = (f32[2304]{0:T(1024)S(1)}, f32[2304]{0:T(1024)}, u32[]{:S(2)}) copy-start(f32[2304]{0:T(1024)} %param.8) | copy-start | bytes 27652
Sparse Core Ops, SparseCore 0:
  27.8 63.0 all-gather.1
  309.3 117.3 reduce-scatter.1
